TPU v7x, 256 devices: a whole 4x4x8 slice. The times are simulated.
256 devices in a mesh: grp: 8 (over y_hi, x), frag: 32 (over y_lo, z, core).
Axes of the slice: x: 4, y: 4 (y_hi: 2, y_lo: 2; y = y_hi * 2 + y_lo), z: 8, core: 2. Of those that a mesh axis runs over, the one named last changes fastest.
Arguments:
- density: bfloat16 [256, 9216], P('frag'), may hold values from -0.1 to 1, as said below
- fock_blocks: bfloat16 [256, 9216], P('frag'), may hold values from -8 to 8, as said below
- coupling: bfloat16 [1024, 9216], P(('grp', 'frag')), may hold values from -1.796875 to 1.796875
- dimer_pairs: int32 [1024, 2], P(('grp', 'frag')), may hold values from 0 to 255, as said below
- atom_counts: int32 [256], P('frag'), may hold values from 8 to 16
- nuclear_charge: float32 [4096], P('frag'), may hold values from 4 to 12
- coords: float32 [3, 4096], P(None, 'frag'), may hold values from -120 to 120
Outputs:
- density_correction: float32 [256, 9216], P('frag')
- dimer_energy: float32 [1024], P(('grp', 'frag'))
- total_energy: float32 [], replicated
Inputs may be any that keep to these rules, and one draw needn't show every extreme that they name: `dimer_pairs`: dimer d has fragments I < J; I // 8 == (d // 4) % 32, and J // 8 lies between I // 8 and I // 8 + 3. `density`: each row is a symmetric matrix. `fock_blocks`: each row is a symmetric matrix.
All inputs are finite; a program needn't handle non-finite values. Where the computation divides by a largest or mean magnitude, that divisor is 1e-20 or more.
Results may differ from a plain program's by a relative error of at most 0.0018.
Values may be sent and summed in bfloat16 or wider, within the bound.
No kernel may reach another device: no remote copies, remote signals or barrier semaphores. Data moves between devices by JAX's collectives and lax.ppermute only.
A program may use at most 64 MiB of HBM per device.

v0:
```python
import jax
import jax.numpy as jnp
from jax import lax
from jax.sharding import Mesh
from jax.sharding import PartitionSpec as P

NB = 96
NA = 16
REACH = 3
PURIF = 12
FRAG = ("frag_0", "frag_1", "frag_2")
GRP = ("grp_0", "grp_1")
GRP_FRAG = ("grp_0", "grp_1", "frag_0", "frag_1", "frag_2")
FULL_PRECISION = lax.Precision.HIGHEST


def from_everyone(value, axis):
    copies = jnp.broadcast_to(value, (lax.axis_size(axis), *value.shape))
    return lax.all_to_all(copies, axis, split_axis=0, concat_axis=0, tiled=True)


def joined_along(pieces, dim):
    shape = list(pieces.shape[1:])
    shape[dim] *= pieces.shape[0]
    return jnp.moveaxis(pieces, 0, dim).reshape(shape)


def collect(value, axis, dim):
    pieces = from_everyone(value, axis)
    return joined_along(pieces, dim)


def from_behind(value, axis, steps):
    count = lax.axis_size(axis)
    first, last = (max(0, -steps), min(count, count - steps))
    return lax.ppermute(value, axis, [(source, source + steps) for source in range(first, last)])


def in_blocks(value, dim, peers):
    shape = value.shape
    pieces = value.reshape(*shape[:dim], peers, shape[dim] // peers, *shape[dim + 1 :])
    return jnp.moveaxis(pieces, dim, 0)


def sent_and_summed(value, axis, dim):
    pieces = in_blocks(value, dim, lax.axis_size(axis))
    arrived = lax.all_to_all(pieces, axis, split_axis=0, concat_axis=0, tiled=True)
    return arrived.sum(axis=0)


def by_axis(value, axes):
    for axis in axes:
        value = lax.psum(value, axis)
    return value


def basis_atoms(count_real):
    basis_index = jnp.arange(NB, dtype=jnp.float32)[None, :, None]
    atom_index = jnp.arange(NA, dtype=jnp.float32)[None, None, :]
    scaled = basis_index * count_real[:, None, None]
    inside = jnp.logical_and(atom_index * NB <= scaled, scaled < (atom_index + 1.0) * NB)
    return inside.astype(jnp.float32)


def atom_table(density, nuclear_charge, atom_counts, coords):
    frag_count = density.shape[0]
    count_real = atom_counts.astype(jnp.float32)
    owners = basis_atoms(count_real)
    blocks = density.reshape(frag_count, NB, NB).astype(jnp.float32)
    on_diagonal = jnp.diagonal(blocks, axis1=1, axis2=2)
    population = 2.0 * jnp.sum(on_diagonal[:, :, None] * owners, axis=1)
    is_live = (jnp.arange(NA, dtype=jnp.float32)[None, :] < count_real[:, None]).astype(jnp.float32)
    charge = is_live * nuclear_charge.reshape(frag_count, NA) - population
    return jnp.concatenate([charge.reshape(1, -1), coords, is_live.reshape(1, -1)], axis=0)


def embed_potential(receivers, pair_ids, atom_rows):
    source_frag = jnp.arange(atom_rows.shape[1], dtype=jnp.int32) // NA
    keep_mask = jnp.logical_and(source_frag != pair_ids[0], source_frag != pair_ids[1]).astype(
        jnp.float32
    )
    offsets = receivers[1:4, :, None] - atom_rows[1:4, None, :]
    distance_sq = jnp.sum(offsets * offsets, axis=0)
    return jnp.sum((keep_mask * atom_rows[0])[None, :] / jnp.sqrt(distance_sq + 1.0), axis=1)


def dimer_solve(dens_pair, fock_pair, coupling_row, potential, count_pair):
    owners = basis_atoms(count_pair)
    site_shift = jnp.sum(owners * potential.reshape(2, 1, NA), axis=2)
    dens_blocks = dens_pair.astype(jnp.float32).reshape(2, NB, NB)
    fock_parts = fock_pair.astype(jnp.float32).reshape(2, NB, NB)
    cross_block = coupling_row.astype(jnp.float32).reshape(NB, NB)
    small_eye = jnp.eye(NB, dtype=jnp.float32)
    top_rows = jnp.concatenate(
        [fock_parts[0] + small_eye * site_shift[0][None, :], cross_block], axis=1
    )
    low_rows = jnp.concatenate(
        [cross_block.T, fock_parts[1] + small_eye * site_shift[1][None, :]], axis=1
    )
    dimer_fock = jnp.concatenate([top_rows, low_rows], axis=0)
    identity = jnp.eye(2 * NB, dtype=jnp.float32)
    centre = jnp.trace(dimer_fock) / (2.0 * NB)
    shifted = dimer_fock - centre * identity
    width = jnp.max(jnp.sum(jnp.abs(shifted), axis=1)) + 1e-06
    start = 0.5 * identity - shifted / (2.0 * width)

    def purify(index, current):
        square = jnp.dot(current, current, precision=FULL_PRECISION)
        return 3.0 * square - 2.0 * jnp.dot(square, current, precision=FULL_PRECISION)

    purified = lax.fori_loop(0, PURIF, purify, start)
    zero_block = jnp.zeros((NB, NB), jnp.float32)
    start_guess = jnp.concatenate(
        [
            jnp.concatenate([dens_blocks[0], zero_block], axis=1),
            jnp.concatenate([zero_block, dens_blocks[1]], axis=1),
        ],
        axis=0,
    )
    energy = jnp.sum((purified - start_guess) * dimer_fock.T)
    changes = jnp.stack([purified[:NB, :NB] - dens_blocks[0], purified[NB:, NB:] - dens_blocks[1]])
    return (changes.reshape(2, NB * NB), energy)


def per_device(density, fock_blocks, coupling, dimer_pairs, atom_counts, nuclear_charge, coords):
    frag_dev = density.shape[0]
    local_rows = atom_table(density, nuclear_charge, atom_counts, coords)
    atom_rows = collect(local_rows, FRAG, 1)
    my_index = lax.axis_index(FRAG)
    dens_list = [density]
    fock_list = [fock_blocks]
    for distance in range(1, REACH + 1):
        got_dens, got_fock = from_behind((density, fock_blocks), FRAG, -distance)
        dens_list.append(got_dens)
        fock_list.append(got_fock)
    held_dens = jnp.concatenate(dens_list, axis=0)
    held_fock = jnp.concatenate(fock_list, axis=0)
    first_row = my_index * frag_dev
    held_index = dimer_pairs - first_row

    def solve_one(pair_ids, row_pair, coupling_row):
        columns = (pair_ids[:, None] * NA + jnp.arange(NA, dtype=jnp.int32)[None, :]).reshape(-1)
        receivers = jnp.take(atom_rows, columns, axis=1)
        potential = embed_potential(receivers, pair_ids, atom_rows)
        count_pair = jnp.sum(receivers[4].reshape(2, NA), axis=1)
        return dimer_solve(
            jnp.take(held_dens, row_pair, axis=0),
            jnp.take(held_fock, row_pair, axis=0),
            coupling_row,
            potential,
            count_pair,
        )

    changes, energies = jax.vmap(solve_one)(dimer_pairs, held_index, coupling)
    held_count = held_dens.shape[0]
    selector = (
        jnp.arange(held_count, dtype=jnp.int32)[:, None] == held_index.reshape(1, -1)
    ).astype(jnp.float32)
    partial_value = jnp.dot(selector, changes.reshape(-1, NB * NB), precision=FULL_PRECISION)
    partial_value = sent_and_summed(partial_value, GRP, 1)
    own_rows = partial_value[:frag_dev]
    for distance in range(1, REACH + 1):
        piece = partial_value[distance * frag_dev : (distance + 1) * frag_dev]
        own_rows = own_rows + from_behind(piece.astype(jnp.bfloat16), FRAG, distance).astype(
            piece.dtype
        )
    own_rows = collect(own_rows, GRP, 1)
    total_energy = by_axis(jnp.sum(energies), GRP_FRAG)
    return (own_rows, energies, total_energy)


def solution(mesh):
    finer = Mesh(
        mesh.devices.reshape(2, 4, 2, 8, 2), ("grp_0", "grp_1", "frag_0", "frag_1", "frag_2")
    )
    return jax.shard_map(
        per_device,
        mesh=finer,
        in_specs=(
            P(FRAG, None),
            P(FRAG, None),
            P(GRP_FRAG, None),
            P(GRP_FRAG, None),
            P(FRAG),
            P(FRAG),
            P(None, FRAG),
        ),
        out_specs=(P(FRAG, None), P(GRP_FRAG), P()),
        check_vma=False,
    )
```

profile of v0, /device:TPU:1, one launch (start us, length us, event | category | flops | bytes accessed | tf_op | source)
XLA Modules:
  0.0 172.8 jit_solution(6586813165077546668)
XLA Ops:
  0.6 5.1 %collective-permute-start = (bf16[8,9216]{1,0:T(8,128)(2,1)}, bf16[8,9216]{1,0:T(8,128)(2,1)S(1)}, u32[]{:S(2)}, u32[]{:S(2)}) collective-permute-start(bf16[8,9216]{1,0:T(8,128)(2,1)} %param.12), channel_id=1, source_target_pairs={{1,0},{2,1},{3,2},{4,3},{5,4},{6,5},{7,6},{8,7},{9,8},{10,9},{11,1... | collective-permute-start | bytes 442376 | tf_op jit(solution)/shard_map/ppermute | solution.py:36
  5.7 1.3 collective-permute-start.1
  7.0 1.3 collective-permute-start.2
  8.3 1.9 %collective-permute-start.3 = (bf16[8,9216]{1,0:T(8,128)(2,1)}, bf16[8,9216]{1,0:T(8,128)(2,1)S(1)}, u32[]{:S(2)}, u32[]{:S(2)}) collective-permute-start(bf16[8,9216]{1,0:T(8,128)(2,1)} %param.11), channel_id=1, source_target_pairs={{1,0},{2,1},{3,2},{4,3},{5,4},{6,5},{7,6},{8,7},{9,8},{10,9},{11,1... | collective-permute-start | bytes 442376 | tf_op jit(solution)/shard_map/ppermute | solution.py:36
  10.3 1.3 collective-permute-start.4
  11.7 3.4 %copy.86 = f32[8,9216]{0,1:T(8,128)} copy(bf16[8,9216]{1,0:T(8,128)(2,1)} %param.11) | data formatting | bytes 442368 | tf_op jit(solution)/shard_map/convert_element_type | solution.py:69
  15.3 2.9 %gather_fusion = f32[96,8]{1,0:T(8,128)S(1)} fusion(f32[8,96,96]{0,2,1:T(8,128)} %bitcast.84, s32[96]{0:T(128)S(1)} %or_bitcast_fusion), kind=kCustom, calls=%fused_computation.2 | custom fusion | bytes 6912 | tf_op jit(solution)/shard_map/jit(diagonal)/gather | solution.py:70
  19.4 15.1 %all-to-all-start = ((f32[32,5,128]{2,1,0:T(8,128)}), f32[32,5,128]{2,1,0:T(8,128)S(1)}, u32[]{:S(2)}, u32[]{:S(2)}) async-start(f32[32,5,128]{2,1,0:T(8,128)} %broadcast_in_dim.37), calls=%async_computation | async-start | bytes 262144 | tf_op jit(solution)/shard_map/all_to_all | solution.py:19
  40.1 1.3 collective-permute-start.5
  42.2 8.3 %collective-permute-done.5 = bf16[8,9216]{1,0:T(8,128)(2,1)S(1)} collective-permute-done((bf16[8,9216]{1,0:T(8,128)(2,1)S(1)}, bf16[8,9216]{1,0:T(8,128)(2,1)S(1)}, u32[]{:S(2)}, u32[]{:S(2)}) %collective-permute-start.5) | collective-permute-done | bytes 147488 | tf_op jit(solution)/shard_map/ppermute | solution.py:36
  53.7 1.5 copy.89
  60.9 23.0 %while.10 = (s32[]{:T(128)}, f32[4,192,192]{2,1,0:T(8,128)S(1)}, s32[]{:T(128)}) while((s32[]{:T(128)}, f32[4,192,192]{2,1,0:T(8,128)S(1)}, s32[]{:T(128)}) %tuple.36), condition=%wide.region_9.11_spmd, body=%wide.region_8.10_spmd.sunk | while | flops 679919616 | bytes 4128813 | solution.py:111
  61.0 0.9 fusion.41
  61.9 0.9 fusion.42
  62.9 0.9 fusion.41
  63.8 0.9 fusion.42
  64.8 0.9 fusion.41
  65.7 0.9 fusion.42
  66.7 0.9 fusion.41
  67.6 0.9 fusion.42
  68.6 0.9 fusion.41
  69.5 0.9 fusion.42
  70.6 0.9 fusion.41
  71.5 0.9 fusion.42
  72.5 0.9 fusion.41
  73.4 0.9 fusion.42
  74.4 0.9 fusion.41
  75.3 0.9 fusion.42
  76.3 0.9 fusion.41
  77.2 0.9 fusion.42
  78.2 0.9 fusion.41
  79.1 0.9 fusion.42
  80.1 0.9 fusion.41
  81.0 0.9 fusion.42
  82.1 0.9 fusion.41
  83.0 0.9 fusion.42
  85.8 22.6 %all_to_all.15 = f32[8,32,1152]{2,1,0:T(8,128)S(1)} all-to-all(f32[8,32,1152]{2,1,0:T(8,128)S(1)} %convolution_bitcast_fusion), channel_id=1, replica_groups=mesh['grp_0'=2,'grp_1'=4,'frag_0'=2,'frag_1'=8,'frag_2'=2] {'grp_0','grp..., dimensions={0} | all-to-all | bytes 2359296 | tf_op jit(solution)/shard_map/all_to_all | solution.py:47
  108.5 5.4 %collective-permute-start.6 = (bf16[8,1152]{1,0:T(8,128)(2,1)S(1)}, bf16[8,1152]{1,0:T(8,128)(2,1)S(1)}, u32[]{:S(2)}, u32[]{:S(2)}) collective-permute-start(bf16[8,1152]{1,0:T(8,128)(2,1)S(1)} %get-tuple-element.33), channel_id=1, source_target_pairs={{0,1},{1,2},{2,3},{3,4},{4,5},{5,6},{6,7},{7,8},{8,9},{9,10},{10,1... | collective-permute-start | bytes 55304 | tf_op jit(solution)/shard_map/ppermute | solution.py:36
  113.8 1.3 collective-permute-start.7
  115.1 6.0 %collective-permute-start.8 = (bf16[8,1152]{1,0:T(8,128)(2,1)S(1)}, bf16[8,1152]{1,0:T(8,128)(2,1)S(1)}, u32[]{:S(2)}, u32[]{:S(2)}) collective-permute-start(bf16[8,1152]{1,0:T(8,128)(2,1)S(1)} %get-tuple-element.34), channel_id=1, source_target_pairs={{0,3},{1,4},{2,5},{3,6},{4,7},{5,8},{6,9},{7,10},{8,11},{9,12},{10... | collective-permute-start | bytes 55304 | tf_op jit(solution)/shard_map/ppermute | solution.py:36
  121.1 0.8 collective-permute-done.8
  122.7 3.4 %all-to-all-start.2 = ((f32[8,8,1152]{2,1,0:T(8,128)}), f32[8,8,1152]{2,1,0:T(8,128)S(1)}, u32[]{:S(2)}, u32[]{:S(2)}) async-start(f32[8,8,1152]{2,1,0:T(8,128)} %broadcast_in_dim.44), calls=%async_computation.2 | async-start | bytes 589824 | tf_op jit(solution)/shard_map/all_to_all | solution.py:19
  126.2 1.0 fusion.21
  127.1 6.0 %psum.35 = f32[]{:T(128)} all-reduce(f32[]{:T(128)} %get-tuple-element.19), channel_id=1, replica_groups=mesh['grp_0'=2,'grp_1'=4,'frag_0'=2,'frag_1'=8,'frag_2'=2] {'grp_0'}, use_global_device_ids=true, to_apply=%region_13.15 | all-reduce | flops 1 | bytes 8 | tf_op jit(solution)/shard_map/psum | solution.py:53
  133.1 9.5 %psum.36 = f32[]{:T(128)} all-reduce(f32[]{:T(128)} %psum.35), channel_id=1, replica_groups=mesh['grp_0'=2,'grp_1'=4,'frag_0'=2,'frag_1'=8,'frag_2'=2] {'grp_1'}, use_global_device_ids=true, to_apply=%region_14.16 | all-reduce | flops 1 | bytes 8 | tf_op jit(solution)/shard_map/psum | solution.py:53
  142.6 4.8 %psum.37 = f32[]{:T(128)} all-reduce(f32[]{:T(128)} %psum.36), channel_id=1, replica_groups=mesh['grp_0'=2,'grp_1'=4,'frag_0'=2,'frag_1'=8,'frag_2'=2] {'frag_0'}, use_global_device_ids=true, to_apply=%region_15.17 | all-reduce | flops 1 | bytes 8 | tf_op jit(solution)/shard_map/psum | solution.py:53
  147.4 13.5 %psum.38 = f32[]{:T(128)} all-reduce(f32[]{:T(128)} %psum.37), channel_id=1, replica_groups=mesh['grp_0'=2,'grp_1'=4,'frag_0'=2,'frag_1'=8,'frag_2'=2] {'frag_1'}, use_global_device_ids=true, to_apply=%region_16.18 | all-reduce | flops 1 | bytes 8 | tf_op jit(solution)/shard_map/psum | solution.py:53
  160.9 11.2 %psum.39 = f32[]{:T(128)} all-reduce(f32[]{:T(128)} %psum.38), channel_id=1, replica_groups=mesh['grp_0'=2,'grp_1'=4,'frag_0'=2,'frag_1'=8,'frag_2'=2] {'frag_2'}, use_global_device_ids=true, to_apply=%region_17.19 | all-reduce | flops 1 | bytes 8 | tf_op jit(solution)/shard_map/psum | solution.py:53
  (150 shorter events, 20.3 us)
Async XLA Ops:
  0.6 39.4 %collective-permute-start = (bf16[8,9216]{1,0:T(8,128)(2,1)}, bf16[8,9216]{1,0:T(8,128)(2,1)S(1)}, u32[]{:S(2)}, u32[]{:S(2)}) collective-permute-start(bf16[8,9216]{1,0:T(8,128)(2,1)} %param.12), channel_id=1, source_target_pairs={{1,0},{2,1},{3,2},{4,3},{5,4},{6,5},{7,6},{8,7},{9,8},{10,9},{11,1... | collective-permute-start | bytes 442376 | tf_op jit(solution)/shard_map/ppermute | solution.py:36
  5.7 35.6 %collective-permute-start.1 = (bf16[8,9216]{1,0:T(8,128)(2,1)}, bf16[8,9216]{1,0:T(8,128)(2,1)S(1)}, u32[]{:S(2)}, u32[]{:S(2)}) collective-permute-start(bf16[8,9216]{1,0:T(8,128)(2,1)} %param.12), channel_id=1, source_target_pairs={{2,0},{3,1},{4,2},{5,3},{6,4},{7,5},{8,6},{9,7},{10,8},{11,9},{12,... | collective-permute-start | bytes 442376 | tf_op jit(solution)/shard_map/ppermute | solution.py:36
  7.0 34.3 %collective-permute-start.2 = (bf16[8,9216]{1,0:T(8,128)(2,1)}, bf16[8,9216]{1,0:T(8,128)(2,1)S(1)}, u32[]{:S(2)}, u32[]{:S(2)}) collective-permute-start(bf16[8,9216]{1,0:T(8,128)(2,1)} %param.12), channel_id=1, source_target_pairs={{3,0},{4,1},{5,2},{6,3},{7,4},{8,5},{9,6},{10,7},{11,8},{12,9},{13... | collective-permute-start | bytes 442376 | tf_op jit(solution)/shard_map/ppermute | solution.py:36
  8.3 33.8 %collective-permute-start.3 = (bf16[8,9216]{1,0:T(8,128)(2,1)}, bf16[8,9216]{1,0:T(8,128)(2,1)S(1)}, u32[]{:S(2)}, u32[]{:S(2)}) collective-permute-start(bf16[8,9216]{1,0:T(8,128)(2,1)} %param.11), channel_id=1, source_target_pairs={{1,0},{2,1},{3,2},{4,3},{5,4},{6,5},{7,6},{8,7},{9,8},{10,9},{11,1... | collective-permute-start | bytes 442376 | tf_op jit(solution)/shard_map/ppermute | solution.py:36
  10.3 31.9 %collective-permute-start.4 = (bf16[8,9216]{1,0:T(8,128)(2,1)}, bf16[8,9216]{1,0:T(8,128)(2,1)S(1)}, u32[]{:S(2)}, u32[]{:S(2)}) collective-permute-start(bf16[8,9216]{1,0:T(8,128)(2,1)} %param.11), channel_id=1, source_target_pairs={{2,0},{3,1},{4,2},{5,3},{6,4},{7,5},{8,6},{9,7},{10,8},{11,9},{12,... | collective-permute-start | bytes 442376 | tf_op jit(solution)/shard_map/ppermute | solution.py:36
  11.6 6.7 %copy-start.13 = (f32[16]{0:T(128)}, f32[16]{0:T(128)S(1)}, u32[]{:S(2)}) copy-start(f32[16]{0:T(128)S(1)} %get-tuple-element.44) | copy-start | bytes 196
  11.6 6.7 %copy-start.15 = (f32[16]{0:T(128)}, f32[16]{0:T(128)S(1)}, u32[]{:S(2)}) copy-start(f32[16]{0:T(128)S(1)} %get-tuple-element.45) | copy-start | bytes 196
  11.6 3.5 %copy-start.18 = (s32[8]{0:T(128)S(1)}, s32[8]{0:T(128)}, u32[]{:S(2)}) copy-start(s32[8]{0:T(128)} %param.15) | copy-start | bytes 100
  11.6 7.1 %copy-start.17 = (f32[128]{0:T(128)S(1)}, f32[128]{0:T(128)}, u32[]{:S(2)}) copy-start(f32[128]{0:T(128)} %param.16) | copy-start | bytes 1540
  11.6 7.1 %copy-start.12 = (f32[3,128]{1,0:T(4,128)S(1)}, f32[3,128]{1,0:T(4,128)}, u32[]{:S(2)}) copy-start(f32[3,128]{1,0:T(4,128)} %param.17) | copy-start | bytes 4612
  11.6 22.9 %copy-start.8 = (s32[4,2]{0,1:T(2,128)S(1)}, s32[4,2]{0,1:T(2,128)}, u32[]{:S(2)}) copy-start(s32[4,2]{0,1:T(2,128)} %param.14) | copy-start | bytes 100
  11.7 26.8 %copy-start.6 = (bf16[4,9216]{1,0:T(4,128)(2,1)S(1)}, bf16[4,9216]{1,0:T(4,128)(2,1)}, u32[]{:S(2)}) copy-start(bf16[4,9216]{1,0:T(4,128)(2,1)} %param.13) | copy-start | bytes 221188
  15.1 25.0 %copy-start.2 = (bf16[8,9216]{1,0:T(8,128)(2,1)S(1)}, bf16[8,9216]{1,0:T(8,128)(2,1)}, u32[]{:S(2)}) copy-start(bf16[8,9216]{1,0:T(8,128)(2,1)} %param.11) | copy-start | bytes 442372
  15.1 26.3 %copy-start.5 = (bf16[8,9216]{1,0:T(8,128)(2,1)S(1)}, bf16[8,9216]{1,0:T(8,128)(2,1)}, u32[]{:S(2)}) copy-start(bf16[8,9216]{1,0:T(8,128)(2,1)} %param.12) | copy-start | bytes 442372
  19.4 33.0 %all-to-all-start = ((f32[32,5,128]{2,1,0:T(8,128)}), f32[32,5,128]{2,1,0:T(8,128)S(1)}, u32[]{:S(2)}, u32[]{:S(2)}) async-start(f32[32,5,128]{2,1,0:T(8,128)} %broadcast_in_dim.37), calls=%async_computation | async-start | bytes 262144 | tf_op jit(solution)/shard_map/all_to_all | solution.py:19
  40.1 10.4 %collective-permute-start.5 = (bf16[8,9216]{1,0:T(8,128)(2,1)S(1)}, bf16[8,9216]{1,0:T(8,128)(2,1)S(1)}, u32[]{:S(2)}, u32[]{:S(2)}) collective-permute-start(bf16[8,9216]{1,0:T(8,128)(2,1)S(1)} %copy-done.2), channel_id=1, source_target_pairs={{3,0},{4,1},{5,2},{6,3},{7,4},{8,5},{9,6},{10,7},{11,8},{12,9},{13... | collective-permute-start | bytes 442376 | tf_op jit(solution)/shard_map/ppermute | solution.py:36
  52.4 1.3 copy-start
  56.1 2.4 %copy-start.7 = (f32[4096]{0:T(1024)S(1)}, f32[4096]{0:T(1024)}, u32[]{:S(2)}) copy-start(f32[4096]{0:T(1024)} %slice_bitcast_fusion.3) | copy-start | bytes 49156
  56.1 2.4 %copy-start.10 = (s32[4]{0:T(128)S(1)}, s32[4]{0:T(128)}, u32[]{:S(2)}) copy-start(s32[4]{0:T(128)} %get-tuple-element.38) | copy-start | bytes 52
  56.1 2.4 %copy-start.11 = (s32[4]{0:T(128)S(1)}, s32[4]{0:T(128)}, u32[]{:S(2)}) copy-start(s32[4]{0:T(128)} %get-tuple-element.39) | copy-start | bytes 52
  58.4 0.9 copy-start.14
  58.4 0.9 copy-start.16
  58.4 1.0 copy-start.4
  58.6 1.0 copy-start.3
  59.5 1.1 copy-start.1
  84.3 0.7 copy-start.9
  108.5 12.6 %collective-permute-start.6 = (bf16[8,1152]{1,0:T(8,128)(2,1)S(1)}, bf16[8,1152]{1,0:T(8,128)(2,1)S(1)}, u32[]{:S(2)}, u32[]{:S(2)}) collective-permute-start(bf16[8,1152]{1,0:T(8,128)(2,1)S(1)} %get-tuple-element.33), channel_id=1, source_target_pairs={{0,1},{1,2},{2,3},{3,4},{4,5},{5,6},{6,7},{7,8},{8,9},{9,10},{10,1... | collective-permute-start | bytes 55304 | tf_op jit(solution)/shard_map/ppermute | solution.py:36
  113.8 7.3 %collective-permute-start.7 = (bf16[8,1152]{1,0:T(8,128)(2,1)S(1)}, bf16[8,1152]{1,0:T(8,128)(2,1)S(1)}, u32[]{:S(2)}, u32[]{:S(2)}) collective-permute-start(bf16[8,1152]{1,0:T(8,128)(2,1)S(1)} %get-tuple-element.35), channel_id=1, source_target_pairs={{0,2},{1,3},{2,4},{3,5},{4,6},{5,7},{6,8},{7,9},{8,10},{9,11},{10,... | collective-permute-start | bytes 55304 | tf_op jit(solution)/shard_map/ppermute | solution.py:36
  115.1 6.8 %collective-permute-start.8 = (bf16[8,1152]{1,0:T(8,128)(2,1)S(1)}, bf16[8,1152]{1,0:T(8,128)(2,1)S(1)}, u32[]{:S(2)}, u32[]{:S(2)}) collective-permute-start(bf16[8,1152]{1,0:T(8,128)(2,1)S(1)} %get-tuple-element.34), channel_id=1, source_target_pairs={{0,3},{1,4},{2,5},{3,6},{4,7},{5,8},{6,9},{7,10},{8,11},{9,12},{10... | collective-permute-start | bytes 55304 | tf_op jit(solution)/shard_map/ppermute | solution.py:36
  122.7 49.4 %all-to-all-start.2 = ((f32[8,8,1152]{2,1,0:T(8,128)}), f32[8,8,1152]{2,1,0:T(8,128)S(1)}, u32[]{:S(2)}, u32[]{:S(2)}) async-start(f32[8,8,1152]{2,1,0:T(8,128)} %broadcast_in_dim.44), calls=%async_computation.2 | async-start | bytes 589824 | tf_op jit(solution)/shard_map/all_to_all | solution.py:19
where the time goes:
time: 174 us; the launch traced here: 173 us
  blocking collectives  67.5 us (39%)
  starting transfers between devices  43.3 us (25%)
  matrix products  22.6 us (13%)
  local copies, waits for them, and re-layouts  19.7 us (11%)
  waiting for transfers between devices  9.16 us (5%)
  other arithmetic  8.75 us (5%)
    psum x5, blocking collectives, by_axis(): value = lax.psum(value, axis)  44.9 us
    ppermute x9, starting transfers between devices, from_behind(): lax.ppermute(value, axis, [(source, source + steps) for source in range(f...  24.8 us
    all_to_all x1, blocking collectives, sent_and_summed(): lax.all_to_all(pieces, axis, split_axis=0, concat_axis=0, tiled=True)  22.6 us
    all_to_all x2, starting transfers between devices, from_everyone(): return lax.all_to_all(copies, axis, split_axis=0, concat_axis=0, tiled=True)  18.5 us
    dot_general x12, matrix products, purify(): jnp.dot(square, current, precision=FULL_PRECISION)  11.2 us
    dot_general x12, matrix products, purify(): square = jnp.dot(current, current, precision=FULL_PRECISION)  10.7 us
    ppermute x9, waiting for transfers between devices, from_behind(): lax.ppermute(value, axis, [(source, source + steps) for source in range(f...  9.15 us
  transfers between devices with their start and end apart: 11, of which 2 were waited for; matrix products, arithmetic and copies ran while one was open for 10% of the time, Pallas kernels for 0%

commit v1 on v0

--- a/solution.py
+++ b/solution.py
@@ -50,7 +50,7 @@
 
 def by_axis(value, axes):
     for axis in axes:
-        value = lax.psum(value, axis)
+        value = jnp.sum(lax.all_gather(value, axis), axis=0)
     return value
 
 

time: 174 us -> 184 us (1.057)
  local copies, waits for them, and re-layouts: 19.7 us -> 30.2 us
  blocking collectives: 67.5 us -> 64.3 us
  other arithmetic: 8.75 us -> 11.8 us
    psum x5 -> x0, blocking collectives: 44.9 us -> none  [by_axis(): value = lax.psum(value, axis)]
    unnamed x0 -> x5, blocking collectives: none -> 41.7 us
    unnamed x43 -> x68, local copies, waits for them, and re-layouts: 2.74 us -> 13.3 us
    reduce_sum x0 -> x5, other arithmetic: none -> 3.02 us  [by_axis(): value = jnp.sum(lax.all_gather(value, axis), axis=0)]
  transfers between devices with their start and end apart: 11 -> 11, of which waited for: 2 -> 2; matrix products, arithmetic and copies ran while one was open for 10% -> 17% of each run, Pallas kernels for 0% -> 0%
where the time goes in v1:
time: 184 us; the launch traced here: 183 us
  blocking collectives  64.3 us (35%)
  starting transfers between devices  43.5 us (24%)
  local copies, waits for them, and re-layouts  30.2 us (16%)
  matrix products  22.6 us (12%)
  other arithmetic  11.8 us (6%)
  waiting for transfers between devices  9.16 us (5%)
    unnamed x5, blocking collectives  41.7 us
    ppermute x9, starting transfers between devices, from_behind(): lax.ppermute(value, axis, [(source, source + steps) for source in range(f...  24.8 us
    all_to_all x1, blocking collectives, sent_and_summed(): lax.all_to_all(pieces, axis, split_axis=0, concat_axis=0, tiled=True)  22.6 us
    all_to_all x2, starting transfers between devices, from_everyone(): return lax.all_to_all(copies, axis, split_axis=0, concat_axis=0, tiled=True)  18.7 us
    unnamed x68, local copies, waits for them, and re-layouts  13.3 us
    dot_general x12, matrix products, purify(): jnp.dot(square, current, precision=FULL_PRECISION)  11.2 us
    dot_general x12, matrix products, purify(): square = jnp.dot(current, current, precision=FULL_PRECISION)  10.7 us
    ppermute x9, waiting for transfers between devices, from_behind(): lax.ppermute(value, axis, [(source, source + steps) for source in range(f...  9.15 us
  transfers between devices with their start and end apart: 11, of which 2 were waited for; matrix products, arithmetic and copies ran while one was open for 17% of the time, Pallas kernels for 0%

profile of v1, /device:TPU:1, one launch (start us, length us, event | category | flops | bytes accessed | tf_op | source)
XLA Modules:
  0.0 183.4 jit_solution(1791864376946041792)
XLA Ops:
  0.6 5.1 %collective-permute-start = (bf16[8,9216]{1,0:T(8,128)(2,1)}, bf16[8,9216]{1,0:T(8,128)(2,1)S(1)}, u32[]{:S(2)}, u32[]{:S(2)}) collective-permute-start(bf16[8,9216]{1,0:T(8,128)(2,1)} %param.12), channel_id=1, source_target_pairs={{1,0},{2,1},{3,2},{4,3},{5,4},{6,5},{7,6},{8,7},{9,8},{10,9},{11,1... | collective-permute-start | bytes 442376 | tf_op jit(solution)/shard_map/ppermute | solution.py:36
  5.7 1.3 collective-permute-start.1
  7.0 1.3 collective-permute-start.2
  8.3 1.9 %collective-permute-start.3 = (bf16[8,9216]{1,0:T(8,128)(2,1)}, bf16[8,9216]{1,0:T(8,128)(2,1)S(1)}, u32[]{:S(2)}, u32[]{:S(2)}) collective-permute-start(bf16[8,9216]{1,0:T(8,128)(2,1)} %param.11), channel_id=1, source_target_pairs={{1,0},{2,1},{3,2},{4,3},{5,4},{6,5},{7,6},{8,7},{9,8},{10,9},{11,1... | collective-permute-start | bytes 442376 | tf_op jit(solution)/shard_map/ppermute | solution.py:36
  10.3 1.3 collective-permute-start.4
  11.7 3.4 %copy.86 = f32[8,9216]{0,1:T(8,128)} copy(bf16[8,9216]{1,0:T(8,128)(2,1)} %param.11) | data formatting | bytes 442368 | tf_op jit(solution)/shard_map/convert_element_type | solution.py:69
  15.3 2.9 %gather_fusion = f32[96,8]{1,0:T(8,128)S(1)} fusion(f32[8,96,96]{0,2,1:T(8,128)} %bitcast.94, s32[96]{0:T(128)S(1)} %or_bitcast_fusion), kind=kCustom, calls=%fused_computation.2 | custom fusion | bytes 6912 | tf_op jit(solution)/shard_map/jit(diagonal)/gather | solution.py:70
  19.4 15.1 %all-to-all-start = ((f32[32,5,128]{2,1,0:T(8,128)}), f32[32,5,128]{2,1,0:T(8,128)S(1)}, u32[]{:S(2)}, u32[]{:S(2)}) async-start(f32[32,5,128]{2,1,0:T(8,128)} %broadcast_in_dim.37), calls=%async_computation | async-start | bytes 262144 | tf_op jit(solution)/shard_map/all_to_all | solution.py:19
  40.1 1.3 collective-permute-start.5
  42.2 8.3 %collective-permute-done.5 = bf16[8,9216]{1,0:T(8,128)(2,1)S(1)} collective-permute-done((bf16[8,9216]{1,0:T(8,128)(2,1)S(1)}, bf16[8,9216]{1,0:T(8,128)(2,1)S(1)}, u32[]{:S(2)}, u32[]{:S(2)}) %collective-permute-start.5) | collective-permute-done | bytes 147488 | tf_op jit(solution)/shard_map/ppermute | solution.py:36
  53.7 1.5 copy.89
  60.9 23.0 %while.10 = (s32[]{:T(128)}, f32[4,192,192]{2,1,0:T(8,128)S(1)}, s32[]{:T(128)}) while((s32[]{:T(128)}, f32[4,192,192]{2,1,0:T(8,128)S(1)}, s32[]{:T(128)}) %tuple.36), condition=%wide.region_9.11_spmd, body=%wide.region_8.10_spmd.sunk | while | flops 679919616 | bytes 4128813 | solution.py:111
  61.0 0.9 fusion.41
  61.9 0.9 fusion.42
  62.9 0.9 fusion.41
  63.8 0.9 fusion.42
  64.8 0.9 fusion.41
  65.7 0.9 fusion.42
  67.6 0.9 fusion.42
  68.6 0.9 fusion.41
  69.5 0.9 fusion.42
  71.5 0.9 fusion.42
  72.5 0.9 fusion.41
  73.4 0.9 fusion.42
  75.3 0.9 fusion.42
  76.3 0.9 fusion.41
  77.2 0.9 fusion.42
  78.2 0.9 fusion.41
  79.1 0.9 fusion.42
  81.0 0.9 fusion.42
  82.1 0.9 fusion.41
  83.0 0.9 fusion.42
  85.8 22.6 %all_to_all.15 = f32[8,32,1152]{2,1,0:T(8,128)S(1)} all-to-all(f32[8,32,1152]{2,1,0:T(8,128)S(1)} %convolution_bitcast_fusion), channel_id=1, replica_groups=mesh['grp_0'=2,'grp_1'=4,'frag_0'=2,'frag_1'=8,'frag_2'=2] {'grp_0','grp..., dimensions={0} | all-to-all | bytes 2359296 | tf_op jit(solution)/shard_map/all_to_all | solution.py:47
  108.5 5.4 %collective-permute-start.6 = (bf16[8,1152]{1,0:T(8,128)(2,1)S(1)}, bf16[8,1152]{1,0:T(8,128)(2,1)S(1)}, u32[]{:S(2)}, u32[]{:S(2)}) collective-permute-start(bf16[8,1152]{1,0:T(8,128)(2,1)S(1)} %get-tuple-element.33), channel_id=1, source_target_pairs={{0,1},{1,2},{2,3},{3,4},{4,5},{5,6},{6,7},{7,8},{8,9},{9,10},{10,1... | collective-permute-start | bytes 55304 | tf_op jit(solution)/shard_map/ppermute | solution.py:36
  113.8 1.3 collective-permute-start.7
  115.1 6.0 %collective-permute-start.8 = (bf16[8,1152]{1,0:T(8,128)(2,1)S(1)}, bf16[8,1152]{1,0:T(8,128)(2,1)S(1)}, u32[]{:S(2)}, u32[]{:S(2)}) collective-permute-start(bf16[8,1152]{1,0:T(8,128)(2,1)S(1)} %get-tuple-element.34), channel_id=1, source_target_pairs={{0,3},{1,4},{2,5},{3,6},{4,7},{5,8},{6,9},{7,10},{8,11},{9,12},{10... | collective-permute-start | bytes 55304 | tf_op jit(solution)/shard_map/ppermute | solution.py:36
  122.7 3.6 %all-to-all-start.2 = ((f32[8,8,1152]{2,1,0:T(8,128)}), f32[8,8,1152]{2,1,0:T(8,128)S(1)}, u32[]{:S(2)}, u32[]{:S(2)}) async-start(f32[8,8,1152]{2,1,0:T(8,128)} %broadcast_in_dim.44), calls=%async_computation.2 | async-start | bytes 589824 | tf_op jit(solution)/shard_map/all_to_all | solution.py:19
  127.0 1.0 fusion.21
  128.0 1.4 dynamic-update-slice
  130.1 5.9 %all-reduce.2 = f32[2]{0:T(128)S(1)} all-reduce(f32[2]{0:T(128)S(1)} %dynamic-update-slice), channel_id=1, replica_groups=mesh['grp_0'=2,'grp_1'=4,'frag_0'=2,'frag_1'=8,'frag_2'=2] {'grp_0'}, use_global_device_ids=true, to_apply=%add.2 | all-reduce | flops 2 | bytes 16
  136.6 1.4 dynamic-update-slice.1
  138.7 8.0 %all-reduce.3 = f32[4]{0:T(128)S(1)} all-reduce(f32[4]{0:T(128)S(1)} %dynamic-update-slice.1), channel_id=1, replica_groups=mesh['grp_0'=2,'grp_1'=4,'frag_0'=2,'frag_1'=8,'frag_2'=2] {'grp_1'}, use_global_device_ids=true, to_apply=%add.3 | all-reduce | flops 4 | bytes 32
  147.2 1.4 dynamic-update-slice.2
  149.4 3.8 %all-reduce.4 = f32[2]{0:T(128)S(1)} all-reduce(f32[2]{0:T(128)S(1)} %dynamic-update-slice.2), channel_id=1, replica_groups=mesh['grp_0'=2,'grp_1'=4,'frag_0'=2,'frag_1'=8,'frag_2'=2] {'frag_0'}, use_global_device_ids=true, to_apply=%add.4 | all-reduce | flops 2 | bytes 16
  153.8 1.4 dynamic-update-slice.3
  155.9 12.8 %all-reduce.5 = f32[8]{0:T(128)S(1)} all-reduce(f32[8]{0:T(128)S(1)} %dynamic-update-slice.3), channel_id=1, replica_groups=mesh['grp_0'=2,'grp_1'=4,'frag_0'=2,'frag_1'=8,'frag_2'=2] {'frag_1'}, use_global_device_ids=true, to_apply=%add.5 | all-reduce | flops 8 | bytes 64
  169.3 1.4 dynamic-update-slice.4
  170.8 11.3 %all-reduce.6 = f32[2]{0:T(128)S(1)} all-reduce(f32[2]{0:T(128)S(1)} %dynamic-update-slice.4), channel_id=1, replica_groups=mesh['grp_0'=2,'grp_1'=4,'frag_0'=2,'frag_1'=8,'frag_2'=2] {'frag_2'}, use_global_device_ids=true, to_apply=%add.6 | all-reduce | flops 2 | bytes 16
  (180 shorter events, 31.1 us)
Async XLA Ops:
  0.6 39.4 %collective-permute-start = (bf16[8,9216]{1,0:T(8,128)(2,1)}, bf16[8,9216]{1,0:T(8,128)(2,1)S(1)}, u32[]{:S(2)}, u32[]{:S(2)}) collective-permute-start(bf16[8,9216]{1,0:T(8,128)(2,1)} %param.12), channel_id=1, source_target_pairs={{1,0},{2,1},{3,2},{4,3},{5,4},{6,5},{7,6},{8,7},{9,8},{10,9},{11,1... | collective-permute-start | bytes 442376 | tf_op jit(solution)/shard_map/ppermute | solution.py:36
  5.7 35.6 %collective-permute-start.1 = (bf16[8,9216]{1,0:T(8,128)(2,1)}, bf16[8,9216]{1,0:T(8,128)(2,1)S(1)}, u32[]{:S(2)}, u32[]{:S(2)}) collective-permute-start(bf16[8,9216]{1,0:T(8,128)(2,1)} %param.12), channel_id=1, source_target_pairs={{2,0},{3,1},{4,2},{5,3},{6,4},{7,5},{8,6},{9,7},{10,8},{11,9},{12,... | collective-permute-start | bytes 442376 | tf_op jit(solution)/shard_map/ppermute | solution.py:36
  7.0 34.3 %collective-permute-start.2 = (bf16[8,9216]{1,0:T(8,128)(2,1)}, bf16[8,9216]{1,0:T(8,128)(2,1)S(1)}, u32[]{:S(2)}, u32[]{:S(2)}) collective-permute-start(bf16[8,9216]{1,0:T(8,128)(2,1)} %param.12), channel_id=1, source_target_pairs={{3,0},{4,1},{5,2},{6,3},{7,4},{8,5},{9,6},{10,7},{11,8},{12,9},{13... | collective-permute-start | bytes 442376 | tf_op jit(solution)/shard_map/ppermute | solution.py:36
  8.3 33.8 %collective-permute-start.3 = (bf16[8,9216]{1,0:T(8,128)(2,1)}, bf16[8,9216]{1,0:T(8,128)(2,1)S(1)}, u32[]{:S(2)}, u32[]{:S(2)}) collective-permute-start(bf16[8,9216]{1,0:T(8,128)(2,1)} %param.11), channel_id=1, source_target_pairs={{1,0},{2,1},{3,2},{4,3},{5,4},{6,5},{7,6},{8,7},{9,8},{10,9},{11,1... | collective-permute-start | bytes 442376 | tf_op jit(solution)/shard_map/ppermute | solution.py:36
  10.3 31.9 %collective-permute-start.4 = (bf16[8,9216]{1,0:T(8,128)(2,1)}, bf16[8,9216]{1,0:T(8,128)(2,1)S(1)}, u32[]{:S(2)}, u32[]{:S(2)}) collective-permute-start(bf16[8,9216]{1,0:T(8,128)(2,1)} %param.11), channel_id=1, source_target_pairs={{2,0},{3,1},{4,2},{5,3},{6,4},{7,5},{8,6},{9,7},{10,8},{11,9},{12,... | collective-permute-start | bytes 442376 | tf_op jit(solution)/shard_map/ppermute | solution.py:36
  11.6 6.7 %copy-start.13 = (f32[16]{0:T(128)}, f32[16]{0:T(128)S(1)}, u32[]{:S(2)}) copy-start(f32[16]{0:T(128)S(1)} %get-tuple-element.44) | copy-start | bytes 196
  11.6 6.7 %copy-start.15 = (f32[16]{0:T(128)}, f32[16]{0:T(128)S(1)}, u32[]{:S(2)}) copy-start(f32[16]{0:T(128)S(1)} %get-tuple-element.45) | copy-start | bytes 196
  11.6 3.5 %copy-start.18 = (s32[8]{0:T(128)S(1)}, s32[8]{0:T(128)}, u32[]{:S(2)}) copy-start(s32[8]{0:T(128)} %param.15) | copy-start | bytes 100
  11.6 7.1 %copy-start.17 = (f32[128]{0:T(128)S(1)}, f32[128]{0:T(128)}, u32[]{:S(2)}) copy-start(f32[128]{0:T(128)} %param.16) | copy-start | bytes 1540
  11.6 7.1 %copy-start.12 = (f32[3,128]{1,0:T(4,128)S(1)}, f32[3,128]{1,0:T(4,128)}, u32[]{:S(2)}) copy-start(f32[3,128]{1,0:T(4,128)} %param.17) | copy-start | bytes 4612
  11.6 22.9 %copy-start.8 = (s32[4,2]{0,1:T(2,128)S(1)}, s32[4,2]{0,1:T(2,128)}, u32[]{:S(2)}) copy-start(s32[4,2]{0,1:T(2,128)} %param.14) | copy-start | bytes 100
  11.7 26.8 %copy-start.6 = (bf16[4,9216]{1,0:T(4,128)(2,1)S(1)}, bf16[4,9216]{1,0:T(4,128)(2,1)}, u32[]{:S(2)}) copy-start(bf16[4,9216]{1,0:T(4,128)(2,1)} %param.13) | copy-start | bytes 221188
  15.1 25.0 %copy-start.2 = (bf16[8,9216]{1,0:T(8,128)(2,1)S(1)}, bf16[8,9216]{1,0:T(8,128)(2,1)}, u32[]{:S(2)}) copy-start(bf16[8,9216]{1,0:T(8,128)(2,1)} %param.11) | copy-start | bytes 442372
  15.1 26.3 %copy-start.5 = (bf16[8,9216]{1,0:T(8,128)(2,1)S(1)}, bf16[8,9216]{1,0:T(8,128)(2,1)}, u32[]{:S(2)}) copy-start(bf16[8,9216]{1,0:T(8,128)(2,1)} %param.12) | copy-start | bytes 442372
  19.4 33.0 %all-to-all-start = ((f32[32,5,128]{2,1,0:T(8,128)}), f32[32,5,128]{2,1,0:T(8,128)S(1)}, u32[]{:S(2)}, u32[]{:S(2)}) async-start(f32[32,5,128]{2,1,0:T(8,128)} %broadcast_in_dim.37), calls=%async_computation | async-start | bytes 262144 | tf_op jit(solution)/shard_map/all_to_all | solution.py:19
  40.1 10.4 %collective-permute-start.5 = (bf16[8,9216]{1,0:T(8,128)(2,1)S(1)}, bf16[8,9216]{1,0:T(8,128)(2,1)S(1)}, u32[]{:S(2)}, u32[]{:S(2)}) collective-permute-start(bf16[8,9216]{1,0:T(8,128)(2,1)S(1)} %copy-done.2), channel_id=1, source_target_pairs={{3,0},{4,1},{5,2},{6,3},{7,4},{8,5},{9,6},{10,7},{11,8},{12,9},{13... | collective-permute-start | bytes 442376 | tf_op jit(solution)/shard_map/ppermute | solution.py:36
  52.4 1.3 copy-start
  56.1 2.4 %copy-start.7 = (f32[4096]{0:T(1024)S(1)}, f32[4096]{0:T(1024)}, u32[]{:S(2)}) copy-start(f32[4096]{0:T(1024)} %slice_bitcast_fusion.3) | copy-start | bytes 49156
  56.1 2.4 %copy-start.10 = (s32[4]{0:T(128)S(1)}, s32[4]{0:T(128)}, u32[]{:S(2)}) copy-start(s32[4]{0:T(128)} %get-tuple-element.38) | copy-start | bytes 52
  56.1 2.4 %copy-start.11 = (s32[4]{0:T(128)S(1)}, s32[4]{0:T(128)}, u32[]{:S(2)}) copy-start(s32[4]{0:T(128)} %get-tuple-element.39) | copy-start | bytes 52
  58.4 0.9 copy-start.14
  58.4 0.9 copy-start.16
  58.4 1.0 copy-start.4
  58.6 1.0 copy-start.3
  59.5 1.1 copy-start.1
  84.3 0.7 copy-start.9
  108.4 18.0 %copy-start.23 = (u32[256]{0:T(256)S(1)}, u32[256]{0:T(256)}, u32[]{:S(2)}) copy-start(u32[256]{0:T(256)} %constant.128) | copy-start | bytes 3076
  108.5 12.6 %collective-permute-start.6 = (bf16[8,1152]{1,0:T(8,128)(2,1)S(1)}, bf16[8,1152]{1,0:T(8,128)(2,1)S(1)}, u32[]{:S(2)}, u32[]{:S(2)}) collective-permute-start(bf16[8,1152]{1,0:T(8,128)(2,1)S(1)} %get-tuple-element.33), channel_id=1, source_target_pairs={{0,1},{1,2},{2,3},{3,4},{4,5},{5,6},{6,7},{7,8},{8,9},{9,10},{10,1... | collective-permute-start | bytes 55304 | tf_op jit(solution)/shard_map/ppermute | solution.py:36
  113.8 7.3 %collective-permute-start.7 = (bf16[8,1152]{1,0:T(8,128)(2,1)S(1)}, bf16[8,1152]{1,0:T(8,128)(2,1)S(1)}, u32[]{:S(2)}, u32[]{:S(2)}) collective-permute-start(bf16[8,1152]{1,0:T(8,128)(2,1)S(1)} %get-tuple-element.35), channel_id=1, source_target_pairs={{0,2},{1,3},{2,4},{3,5},{4,6},{5,7},{6,8},{7,9},{8,10},{9,11},{10,... | collective-permute-start | bytes 55304 | tf_op jit(solution)/shard_map/ppermute | solution.py:36
  115.1 6.8 %collective-permute-start.8 = (bf16[8,1152]{1,0:T(8,128)(2,1)S(1)}, bf16[8,1152]{1,0:T(8,128)(2,1)S(1)}, u32[]{:S(2)}, u32[]{:S(2)}) collective-permute-start(bf16[8,1152]{1,0:T(8,128)(2,1)S(1)} %get-tuple-element.34), channel_id=1, source_target_pairs={{0,3},{1,4},{2,5},{3,6},{4,7},{5,8},{6,9},{7,10},{8,11},{9,12},{10... | collective-permute-start | bytes 55304 | tf_op jit(solution)/shard_map/ppermute | solution.py:36
  122.7 6.7 %copy-start.22 = (u32[256]{0:T(256)S(1)}, u32[256]{0:T(256)}, u32[]{:S(2)}) copy-start(u32[256]{0:T(256)} %constant.133) | copy-start | bytes 3076
  122.7 15.3 %copy-start.21 = (u32[256]{0:T(256)S(1)}, u32[256]{0:T(256)}, u32[]{:S(2)}) copy-start(u32[256]{0:T(256)} %constant.138) | copy-start | bytes 3076
  122.7 26.0 %copy-start.20 = (u32[256]{0:T(256)S(1)}, u32[256]{0:T(256)}, u32[]{:S(2)}) copy-start(u32[256]{0:T(256)} %constant.143) | copy-start | bytes 3076
  122.7 32.5 %copy-start.19 = (u32[256]{0:T(256)S(1)}, u32[256]{0:T(256)}, u32[]{:S(2)}) copy-start(u32[256]{0:T(256)} %constant.148) | copy-start | bytes 3076
  122.7 59.9 %all-to-all-start.2 = ((f32[8,8,1152]{2,1,0:T(8,128)}), f32[8,8,1152]{2,1,0:T(8,128)S(1)}, u32[]{:S(2)}, u32[]{:S(2)}) async-start(f32[8,8,1152]{2,1,0:T(8,128)} %broadcast_in_dim.44), calls=%async_computation.2 | async-start | bytes 589824 | tf_op jit(solution)/shard_map/all_to_all | solution.py:19
